TPU v7x, 32 devices: a whole 2x2x4 slice. The times are simulated.
32 devices in a mesh: tile: 16 (over z, y, core), shell: 2 (over x).
Axes of the slice: x: 2, y: 2, z: 4, core: 2. Of those that a mesh axis runs over, the one named last changes fastest.
Arguments:
- particles: bfloat16 [512, 2, 32768], P('tile', None, 'shell'), may hold values from -40 to 40
- projections: bfloat16 [512, 2, 32768], P('tile', None, 'shell'), may hold values from -6 to 6
- noise_weight: float32 [32768], P('shell'), may hold values from 0.001 to 0.012
- tile_list: int32 [512, 4], P('tile'), may hold values from 0 to 15, all different within a row; in each aligned block of 32 rows (0 to 31, 32 to 63, ...) at most 16 rows name the same one
- ori_start: int32 [512, 4], P('tile'), may hold values from 0 to 31
- shifts: int32 [512, 2], P('tile'), may hold values from -8 to 8
- defocus_bin: int32 [512], P('tile'), may hold values from 0 to 15
Outputs:
- posterior: float32 [512, 9, 64], P('tile')
- log_evidence: float32 [512], P('tile')
Inputs may be any that keep to these rules, and one draw needn't show every extreme that they name: `tile_list`: the 4 tiles of one particle differ, and among the particles of one index of tile no tile is named more than 16 times, a count reached.
All inputs are finite; a program needn't handle non-finite values.
Results may differ from a plain program's by a relative error of at most 0.0035.
Values may be sent and summed in bfloat16 or wider, within the bound.
A program may use at most 192 MiB of HBM per device.

v0:
```python
import math

import jax
import jax.numpy as jnp
from jax import lax
from jax.sharding import PartitionSpec as P

BOX = 256
NBIN = 16
TSIDE = 3


wave_length = 0.0197
aberration = 27000000.0
amplitude = 0.1
b_factor = 20.0
defocus_base = 5000.0
defocus_step = 500.0


def frequencies(first_index, span_count):
    flat_index = first_index + jnp.arange(span_count, dtype=jnp.int32)
    freq_x = flat_index // BOX
    freq_y = flat_index % BOX - BOX // 2
    return (freq_x, freq_y)


def ctf_table(freq_x, freq_y, bins_count):
    scaled_x = freq_x.astype(jnp.float32) / BOX
    scaled_y = freq_y.astype(jnp.float32) / BOX
    radius_sq = scaled_x * scaled_x + scaled_y * scaled_y
    defocus = defocus_base + defocus_step * jnp.arange(bins_count, dtype=jnp.float32)[:, None]
    aberr_phase = (
        math.pi * wave_length * defocus * radius_sq[None, :]
        - 0.5 * math.pi * aberration * wave_length**3 * radius_sq[None, :] ** 2
    )
    envelope = jnp.exp(-0.25 * b_factor * radius_sq)[None, :]
    return (
        -(math.sqrt(1.0 - amplitude**2) * jnp.sin(aberr_phase) + amplitude * jnp.cos(aberr_phase))
        * envelope
    )


def rotation(freq_x, freq_y, mult_x, mult_y):
    phase_turns = jnp.mod(freq_x * mult_x + freq_y * mult_y, BOX)
    angles = phase_turns.astype(jnp.float32) * (2.0 * math.pi / BOX)
    return (jnp.cos(angles), jnp.sin(angles))


def pick_rows(bin_index, lookup):
    one_hot = (bin_index[:, None] == jnp.arange(lookup.shape[0], dtype=jnp.int32)[None, :]).astype(
        jnp.float32
    )
    return jnp.dot(
        one_hot, lookup, precision=lax.Precision.HIGHEST, preferred_element_type=jnp.float32
    )


def prepare(particles, weight, ctf_rows, shifts, freq_x, freq_y):
    values = particles.astype(jnp.float32)
    real_part = values[:, 0]
    imag_part = values[:, 1]
    cosine, sine_value = rotation(freq_x[None, :], freq_y[None, :], shifts[:, 0:1], shifts[:, 1:2])
    moved_real = real_part * cosine + imag_part * sine_value
    moved_imag = imag_part * cosine - real_part * sine_value
    factor = weight[None, :] * ctf_rows
    weighted = jnp.stack([factor * moved_real, factor * moved_imag], axis=1).astype(jnp.bfloat16)
    energy = jnp.sum(weight[None, :] * (real_part * real_part + imag_part * imag_part), axis=1)
    return (weighted, energy)


def shifted_tables(projections, freq_x, freq_y):
    offsets = jnp.arange(TSIDE, dtype=jnp.int32) - TSIDE // 2
    mult_x = jnp.repeat(offsets, TSIDE)[:, None]
    mult_y = jnp.tile(offsets, TSIDE)[:, None]
    cosine, sine_value = rotation(freq_x[None, :], freq_y[None, :], mult_x, mult_y)
    cosine = cosine[:, None, :]
    sine_value = sine_value[:, None, :]
    proj_real = projections[:, 0].astype(jnp.float32)[None, :, :]
    proj_imag = projections[:, 1].astype(jnp.float32)[None, :, :]
    moved_real = proj_real * cosine - proj_imag * sine_value
    moved_imag = proj_imag * cosine + proj_real * sine_value
    stacked = jnp.stack([moved_real, moved_imag], axis=2).astype(jnp.bfloat16)
    return stacked.reshape(TSIDE * TSIDE * projections.shape[0], -1)


def slot_scores(slot_rows, bin_index, projections, weight, ctf, freq_x, freq_y):
    orient_count = projections.shape[0]
    lookup = shifted_tables(projections, freq_x, freq_y)
    cross_term = lax.dot_general(
        slot_rows, lookup, (((1,), (1,)), ((), ())), preferred_element_type=jnp.float32
    )
    cross_term = cross_term.reshape(slot_rows.shape[0], TSIDE * TSIDE, orient_count)
    proj_values = projections.astype(jnp.float32)
    magnitude = proj_values[:, 0] * proj_values[:, 0] + proj_values[:, 1] * proj_values[:, 1]
    weighted_ctf = weight[None, :] * ctf * ctf
    power = lax.dot_general(
        weighted_ctf,
        magnitude,
        (((1,), (1,)), ((), ())),
        precision=lax.Precision.HIGHEST,
        preferred_element_type=jnp.float32,
    )
    power_rows = pick_rows(bin_index, power)
    return cross_term - 0.5 * power_rows[:, None, :]


def window(scores, starts, orient_count):
    orient_index = jnp.mod(
        starts[:, None] + jnp.arange(orient_count // 2, dtype=jnp.int32)[None, :], orient_count
    )
    return jnp.take_along_axis(scores, orient_index[:, None, :], axis=2)


def slot_layout(tile_ids, tile_count, capacity):
    positions = jnp.arange(tile_ids.shape[0], dtype=jnp.int32)
    earlier_same = (tile_ids[:, None] == tile_ids[None, :]) & (
        positions[None, :] < positions[:, None]
    )
    slot_rank = jnp.sum(earlier_same.astype(jnp.int32), axis=1)
    slot_index = tile_ids * capacity + slot_rank
    matches = slot_index[None, :] == jnp.arange(tile_count * capacity, dtype=jnp.int32)[:, None]
    slot_owner = jnp.sum(jnp.where(matches, positions[None, :] + 1, 0), axis=1) - 1
    return (slot_index, slot_owner)


def finish(scores, energy_sum):
    scored = scores - 0.5 * energy_sum[:, None, None]
    row_peak = jnp.max(scored, axis=(1, 2))
    log_total = row_peak + jnp.log(jnp.sum(jnp.exp(scored - row_peak[:, None, None]), axis=(1, 2)))
    posterior = jnp.exp(scored - log_total[:, None, None])
    return (posterior, log_total)


def per_device(particles, projections, noise_weight, tile_list, ori_start, shifts, defocus_bin):
    tile_count = lax.axis_size("tile")
    band_index = lax.axis_index("shell")
    local_count = particles.shape[0]
    window_count = tile_list.shape[1]
    band_width = particles.shape[2]
    orient_count = projections.shape[0]
    capacity = max(2, (2 * local_count * window_count + tile_count - 1) // tile_count)
    freq_x, freq_y = frequencies(band_index * band_width, band_width)
    ctf = ctf_table(freq_x, freq_y, NBIN)
    weighted, energy = prepare(
        particles, noise_weight, pick_rows(defocus_bin, ctf), shifts, freq_x, freq_y
    )
    weighted = weighted.reshape(local_count, 2 * band_width)
    slot_index, slot_owner = slot_layout(tile_list.reshape(-1), tile_count, capacity)
    occupied = slot_owner >= 0
    item_index = jnp.maximum(slot_owner, 0)
    particle = item_index // window_count
    starts_flat = ori_start.reshape(-1)
    send_rows = jnp.where(
        occupied[:, None], jnp.take(weighted, particle, axis=0), jnp.zeros((), jnp.bfloat16)
    )
    send_rows = send_rows.reshape(tile_count, capacity, 2 * band_width)
    send_labels = jnp.stack(
        [jnp.take(defocus_bin, particle), jnp.take(starts_flat, item_index)], axis=1
    )
    send_labels = send_labels.astype(jnp.bfloat16).reshape(tile_count, capacity, 2)
    payload = lax.all_to_all(send_rows, "tile", split_axis=0, concat_axis=0, tiled=True)
    labels = lax.all_to_all(send_labels, "tile", split_axis=0, concat_axis=0, tiled=True)
    source_count = payload.shape[0]
    slot_count = payload.shape[1]
    slot_rows = payload.reshape(source_count * slot_count, payload.shape[2])
    label_ints = labels.reshape(source_count * slot_count, 2).astype(jnp.int32)
    partial_value = slot_scores(
        slot_rows, label_ints[:, 0], projections, noise_weight, ctf, freq_x, freq_y
    )
    partial_value = partial_value.reshape(
        source_count, slot_count, partial_value.shape[1], partial_value.shape[2]
    )
    returned = lax.all_to_all(partial_value, "tile", split_axis=0, concat_axis=0, tiled=True)
    candidates = returned.shape[2]
    returned = jnp.take(
        returned.reshape(tile_count * capacity, candidates, returned.shape[3]), slot_index, axis=0
    )
    returned = window(returned, starts_flat, orient_count)
    kept = returned.shape[2]
    returned = returned.reshape(local_count, window_count, candidates, kept)
    scores = jnp.transpose(returned, (0, 2, 1, 3)).reshape(
        local_count, candidates, window_count * kept
    )
    scores, energy_sum = lax.psum((scores, energy), "shell")
    return finish(scores, energy_sum)


def solution(mesh):
    in_specs = (
        P("tile", None, "shell"),
        P("tile", None, "shell"),
        P("shell"),
        P("tile", None),
        P("tile", None),
        P("tile", None),
        P("tile"),
    )
    out_specs = (P("tile", None, None), P("tile"))
    return jax.shard_map(
        per_device, mesh=mesh, in_specs=in_specs, out_specs=out_specs, check_vma=False
    )
```

profile of v0, /device:TPU:0, one launch (start us, length us, event | category | flops | bytes accessed | tf_op | source)
XLA Modules:
  0.0 555.1 jit_solution(15668905499598835098)
XLA Ops:
  7.2 0.8 copy.80
  8.0 0.2 convert_reduce_fusion
  8.4 2.1 fusion.54
  10.5 1.8 fusion.55
  12.3 0.8 copy.79
  13.2 1.9 gather_fusion.1
  15.3 20.1 %compare_select_fusion.7 = s32[256]{0:T(256)S(1)} fusion(s32[256]{0:T(256)S(1)} %bitcast.123, s32[]{:T(128)} %bitcast.13, s32[]{:T(128)} %bitcast.14, s32[]{:T(128)} %bitcast.15, s32[]{:T(128)} %bitcast.16, s32[]{:T(128)} %bitcast.17, s32[]{:T(128)} %bitcast.18, s32[]{:T(128)} %bitcast.19, s32[]{:T(128)} %bitcast.20, s32[]{:T(128)} %bitcast.21, ...), kind=kLoop, calls=%fused_computation.121 | loop fusion | flops 15872 | bytes 2176 | tf_op jit(solution)/shard_map/jit(_take)/gather | solution.py:159
  35.6 0.6 copy.86
  36.2 7.4 %all-to-all-start.1 = ((bf16[16,16,2]{1,2,0:T(2,128)(2,1)}), bf16[16,16,2]{1,2,0:T(2,128)(2,1)S(1)}, u32[]{:S(2)}, u32[]{:S(2)}) async-start(bf16[16,16,2]{1,2,0:T(2,128)(2,1)} %copy.86), calls=%async_computation.1 | async-start | bytes 16384 | tf_op jit(solution)/shard_map/all_to_all | solution.py:163
  44.1 0.8 slice_bitcast_fusion.5
  44.9 2.8 copy_convert_fusion
  47.7 14.6 %fusion.12 = (bf16[32,1,16384]{2,0,1:T(8,128)(2,1)S(1)}, bf16[32,1,16384]{2,0,1:T(8,128)(2,1)S(1)}, f32[32]{0:T(128)S(1)}) fusion(f32[32,2,16384]{2,0,1:T(8,128)S(1)} %copy_convert_fusion, s32[32]{0:T(128)S(1)} %get-tuple-element.30, s32[16384]{0:T(1024)S(1)} %get-tuple-element.64, s32[32]{0:T(128)S(1)} %get-tuple-element.29, ...), kind=kOutput, calls=%fused_computation.38 | convolution fusion | flops 119276000 | bytes 6685248 | tf_op jit(solution)/shard_map/dot_general | solution.py:54
  62.3 0.2 maximum_bitcast_fusion
  62.7 17.2 %gather_fusion = bf16[256,32768]{1,0:T(8,128)(2,1)} fusion(bf16[32,32768]{1,0:T(8,128)(2,1)S(1)} %bitcast.113, s32[1024]{0:T(1024)S(1)} %pad_clamp_fusion.2), kind=kCustom, calls=%fused_computation | custom fusion | bytes 33555456 | tf_op jit(solution)/shard_map/jit(_take)/gather | solution.py:155
  80.0 14.4 %select_select_fusion = bf16[16,16,32768]{2,1,0:T(8,128)(2,1)} fusion(bf16[16,16,32768]{2,1,0:T(8,128)(2,1)} %bitcast.114, pred[16,16]{1,0:T(8,128)(4,1)S(1)} %compare_and_fusion.1, pred[16,16]{1,0:T(8,128)(4,1)S(1)} %ge.64), kind=kLoop, calls=%fused_computation.8 | loop fusion | flops 16777216 | bytes 33554944 | tf_op jit(solution)/shard_map/jit(_where)/select_n | solution.py:154
  94.3 6.3 %all-to-all-start = ((bf16[16,16,32768]{2,1,0:T(8,128)(2,1)}), bf16[16,16,32768]{2,1,0:T(8,128)(2,1)}, u32[]{:S(2)}, u32[]{:S(2)}) async-start(bf16[16,16,32768]{2,1,0:T(8,128)(2,1)} %select_select_fusion), calls=%async_computation | async-start | bytes 33554432 | tf_op jit(solution)/shard_map/all_to_all | solution.py:162
  100.9 4.2 fusion.17
  105.1 4.9 copy_convert_fusion.1
  110.0 0.3 fusion.15
  110.3 41.0 %subtract_convert_fusion = (bf16[9,32,1,16384]{3,2,1,0:T(2,128)(2,1)}, bf16[9,32,1,16384]{3,2,1,0:T(2,128)(2,1)}) fusion(f32[9,16384]{1,0:T(8,128)S(1)} %get-tuple-element.24, f32[32,16384]{1,0:T(8,128)S(1)} %get-tuple-element.22, f32[9,16384]{1,0:T(8,128)S(1)} %get-tuple-element.23, f32[32,16384]{1,0:T(8,128)S(1)} %get-tuple-element.21), kind=kLoop, calls=%fused_computation.6 | loop fusion | flops 37748736 | bytes 24248320 | tf_op jit(solution)/shard_map/convert.8
  151.3 46.0 %pad_maximum_fusion = bf16[9,32,2,16384]{3,2,1,0:T(2,128)(2,1)} fusion(bf16[9,32,1,16384]{3,2,1,0:T(2,128)(2,1)} %get-tuple-element.17, bf16[9,32,1,16384]{3,2,1,0:T(2,128)(2,1)} %get-tuple-element.16), kind=kLoop, calls=%fused_computation.4 | loop fusion | flops 37748736 | bytes 37748736 | tf_op jit(solution)/shard_map/stack | solution.py:83
  197.3 32.7 %convert_element_type.104 = bf16[9,32,32768]{2,1,0:T(8,128)(2,1)} reshape(bf16[9,32,2,16384]{3,2,1,0:T(2,128)(2,1)} %pad_maximum_fusion) | data formatting | bytes 37748736 | tf_op jit(solution)/shard_map/convert_element_type | solution.py:83
  230.4 4.9 psum.15
  235.3 8.9 %fusion.5 = f32[16,32]{1,0:T(8,128)S(1)} fusion(f32[32,2,16384]{2,0,1:T(8,128)} %get-tuple-element.19, f32[16384]{0:T(1024)S(1)} %copy-done.3, f32[16384]{0:T(1024)S(1)} %get-tuple-element.65, f32[16384]{0:T(1024)S(1)} %get-tuple-element.66, f32[16384]{0:T(1024)S(1)} %multiply_add_fusion, f32[16]{0:T(128)S(1)} %add_multiply_fusion), kind=kOutput, calls=%fused_computation.18 | convolution fusion | flops 104595456 | bytes 4458560 | tf_op jit(solution)/shard_map/dot_general | solution.py:97
  244.4 0.3 convolution_multiply_fusion.1
  244.6 152.6 %all-to-all-done = bf16[16,16,32768]{2,1,0:T(8,128)(2,1)} async-done(((bf16[16,16,32768]{2,1,0:T(8,128)(2,1)}), bf16[16,16,32768]{2,1,0:T(8,128)(2,1)}, u32[]{:S(2)}, u32[]{:S(2)}) %all-to-all-start) | async-done | bytes 16777248 | tf_op jit(solution)/shard_map/all_to_all | solution.py:162
  397.2 19.9 %convolution_subtract_fusion = f32[256,9,32]{0,2,1:T(8,128)S(1)} fusion(bf16[256,32768,1]{1,0,2:T(8,128)(2,1)} %bitcast.10, bf16[9,32,32768]{2,1,0:T(8,128)(2,1)} %convert_element_type.104, f32[256,32]{0,1:T(8,128)S(1)} %convolution_multiply_fusion.1), kind=kOutput, calls=%fused_computation.31 | convolution fusion | flops 4831911936 | bytes 35979264 | tf_op jit(solution)/shard_map/dot_general | solution.py:90
  417.2 0.4 copy.89
  417.6 1.2 reshape.709
  418.9 70.2 %all-to-all-start.2 = ((f32[16,1,4608]{2,1,0:T(1,128)}), f32[16,1,4608]{2,1,0:T(1,128)S(1)}, u32[]{:S(2)}, u32[]{:S(2)}) async-start(f32[16,1,4608]{2,1,0:T(1,128)} %reshape.709), calls=%async_computation.2 | async-start | bytes 589824 | tf_op jit(solution)/shard_map/all_to_all | solution.py:174
  489.1 0.2 compare_and_fusion
  489.3 10.3 %all-to-all-done.2 = f32[16,1,4608]{2,1,0:T(1,128)S(1)} async-done(((f32[16,1,4608]{2,1,0:T(1,128)}), f32[16,1,4608]{2,1,0:T(1,128)S(1)}, u32[]{:S(2)}, u32[]{:S(2)}) %all-to-all-start.2) | async-done | bytes 294944 | tf_op jit(solution)/shard_map/all_to_all | solution.py:174
  499.6 0.5 broadcast.1180
  500.1 1.4 reduce
  501.5 0.3 reshape.710
  501.9 0.7 copy.93
  502.7 1.7 gather_fusion.2
  504.4 1.4 broadcast_select_fusion
  505.8 0.8 copy.94
  506.6 13.0 %gather_fusion.3 = f32[2048,9]{1,0:T(8,128)S(1)} fusion(f32[128,9,32]{1,2,0:T(8,128)S(1)} %copy.94, s32[2048]{0:T(1024)S(1)} %reshape.688), kind=kCustom, calls=%fused_computation.3 | custom fusion | bytes 163840 | tf_op jit(solution)/shard_map/jit(take_along_axis)/gather | solution.py:112
  519.7 0.9 copy.95
  520.6 0.2 select_bitcast_fusion
  520.7 0.9 copy.96
  521.7 22.2 %all-reduce.2.cloned.1.call-done = f32[32,9,64]{0,2,1:T(8,128)} async-done(((f32[32,9,64]{0,2,1:T(8,128)}), f32[32,9,64]{0,2,1:T(8,128)}) %all-reduce.2.cloned.1.call-update) | async-done | bytes 73744 | tf_op jit(solution)/shard_map/psum | solution.py:185
  543.9 1.1 subtract_reduce_fusion
  544.9 1.1 exponential_reduce_fusion
  546.0 1.0 subtract_exponential_fusion
  547.0 0.8 copy.97
  (56 shorter events, 2.4 us)
Async XLA Ops:
  36.2 58.1 %all-to-all-start.1 = ((bf16[16,16,2]{1,2,0:T(2,128)(2,1)}), bf16[16,16,2]{1,2,0:T(2,128)(2,1)S(1)}, u32[]{:S(2)}, u32[]{:S(2)}) async-start(bf16[16,16,2]{1,2,0:T(2,128)(2,1)} %copy.86), calls=%async_computation.1 | async-start | bytes 16384 | tf_op jit(solution)/shard_map/all_to_all | solution.py:163
  44.9 2.8 copy-start
  44.9 2.9 copy-start.3
  94.3 302.9 %all-to-all-start = ((bf16[16,16,32768]{2,1,0:T(8,128)(2,1)}), bf16[16,16,32768]{2,1,0:T(8,128)(2,1)}, u32[]{:S(2)}, u32[]{:S(2)}) async-start(bf16[16,16,32768]{2,1,0:T(8,128)(2,1)} %select_select_fusion), calls=%async_computation | async-start | bytes 33554432 | tf_op jit(solution)/shard_map/all_to_all | solution.py:162
  197.3 32.7 %copy-start.1 = (s32[32,4]{0,1:T(4,128)S(1)}, s32[32,4]{0,1:T(4,128)}, u32[]{:S(2)}) copy-start(s32[32,4]{0,1:T(4,128)} %param.10) | copy-start | bytes 1540
  418.9 80.7 %all-to-all-start.2 = ((f32[16,1,4608]{2,1,0:T(1,128)}), f32[16,1,4608]{2,1,0:T(1,128)S(1)}, u32[]{:S(2)}, u32[]{:S(2)}) async-start(f32[16,1,4608]{2,1,0:T(1,128)} %reshape.709), calls=%async_computation.2 | async-start | bytes 589824 | tf_op jit(solution)/shard_map/all_to_all | solution.py:174
  489.1 54.8 %all-reduce.2.cloned.1.call-start = ((), (), s32[]{:S(2)}) async-start(), calls=%async_computation.3 | async-start | bytes 589824 | tf_op jit(solution)/shard_map/psum | solution.py:185
  546.0 1.8 copy-start.2
Sparse Core Ops, SparseCore 0:
  521.8 22.0 all-reduce.1
where the time goes:
time: 565 us; the launch traced here: 555 us
  waiting for transfers between devices  185 us (33%)
  other arithmetic  141 us (25%)
  starting transfers between devices  83.9 us (15%)
  local copies, waits for them, and re-layouts  81.7 us (14%)
  matrix products  43.7 us (8%)
  between operations  14.8 us (3%)
    all_to_all x1, waiting for transfers between devices, per_device(): lax.all_to_all(send_rows, 'tile', split_axis=0, concat_axis=0, tiled=True)  153 us
    all_to_all x1, starting transfers between devices, per_device(): lax.all_to_all(partial_value, 'tile', split_axis=0, concat_axis=0, tiled=...  70.2 us
    another operation x1, other arithmetic, shifted_tables(): stacked = jnp.stack([moved_real, moved_imag], axis=2).astype(jnp.bfloat16)  46 us
    another operation x3, other arithmetic  41.1 us
    convert_element_type x1, local copies, waits for them, and re-layouts, shifted_tables(): stacked = jnp.stack([moved_real, moved_imag], axis=2).astype(jnp.bfloat16)  32.7 us
    psum x1, waiting for transfers between devices, per_device(): scores, energy_sum = lax.psum((scores, energy), 'shell')  22.2 us
    gather x1, other arithmetic, per_device(): jnp.take(defocus_bin, particle)  20.1 us
    dot_general x1, matrix products, slot_scores(): lax.dot_general(slot_rows, lookup, (((1,), (1,)), ((), ())), preferred_el...  19.9 us
  transfers between devices with their start and end apart: 4, of which 3 were waited for; matrix products, arithmetic and copies ran while one was open for 34% of the time, Pallas kernels for 0%

commit v1 on v0

--- a/solution.py
+++ b/solution.py
@@ -1,8 +1,11 @@
+import functools
 import math
 
 import jax
 import jax.numpy as jnp
 from jax import lax
+from jax.experimental import pallas as pl
+from jax.experimental.pallas import tpu as pltpu
 from jax.sharding import PartitionSpec as P
 
 BOX = 256
@@ -132,7 +135,7 @@
     return (posterior, log_total)
 
 
-def per_device(particles, projections, noise_weight, tile_list, ori_start, shifts, defocus_bin):
+def slot_plan(particles, projections, noise_weight, tile_list, ori_start, shifts, defocus_bin):
     tile_count = lax.axis_size("tile")
     band_index = lax.axis_index("shell")
     local_count = particles.shape[0]
@@ -186,6 +189,251 @@
     return finish(scores, energy_sum)
 
 
+SHIFT_MAX = 8
+HIGH = lax.Precision.HIGHEST
+
+
+def round_up(value, step):
+    return (value + step - 1) // step * step
+
+
+def weigh_kernel(part_ref, factor_ref, wave_y_ref, wave_x_ref, weight_ref, out_ref, energy_ref):
+    rows, width = factor_ref.shape
+    lines = width // BOX
+    energy = jnp.zeros((rows, 1), jnp.float32)
+    cos_y = wave_y_ref[:, :BOX]
+    sin_y = wave_y_ref[:, BOX:]
+    for line in range(lines):
+        span = pl.ds(line * BOX, BOX)
+        real_part = part_ref[0, 0, :, span].astype(jnp.float32)
+        imag_part = part_ref[0, 1, :, span].astype(jnp.float32)
+        cos_x = wave_x_ref[:, line : line + 1]
+        sin_x = wave_x_ref[:, lines + line : lines + line + 1]
+        cosine = cos_x * cos_y - sin_x * sin_y
+        sine_value = sin_x * cos_y + cos_x * sin_y
+        factor = factor_ref[:, span]
+        out_ref[:, span] = (factor * (real_part * cosine + imag_part * sine_value)).astype(
+            jnp.bfloat16
+        )
+        out_ref[:, pl.ds(width + line * BOX, BOX)] = (
+            factor * (imag_part * cosine - real_part * sine_value)
+        ).astype(jnp.bfloat16)
+        square = real_part * real_part + imag_part * imag_part
+        energy += jnp.sum(weight_ref[:, span] * square, axis=1, keepdims=True)
+    energy_ref[...] = energy
+
+
+def score_kernel(
+    orients,
+    proj_ref,
+    power_ref,
+    weighted_ref,
+    energy_ref,
+    hot_ref,
+    tiles_ref,
+    starts_ref,
+    cos_ref,
+    sin_ref,
+    out_ref,
+    moved_ref,
+    chosen_ref,
+    final_ref,
+):
+    step = pl.program_id(0)
+    tiles = proj_ref.shape[0]
+    width = proj_ref.shape[3]
+    cands = TSIDE * TSIDE
+    windows = tiles_ref.shape[0]
+    block = cands * orients
+    middle = cands // 2
+    for tile in range(tiles):
+        real_part = proj_ref[tile, 0].astype(jnp.float32)
+        imag_part = proj_ref[tile, 1].astype(jnp.float32)
+
+        def put(cand, real_value, imag_value):
+            rows = pl.ds(tile * block + cand * orients, orients)
+            moved_ref[rows, :width] = real_value.astype(jnp.bfloat16)
+            moved_ref[rows, width:] = imag_value.astype(jnp.bfloat16)
+
+        put(middle, real_part, imag_part)
+        for cand in range(middle):
+            cosine = cos_ref[cand : cand + 1, :]
+            sine_value = sin_ref[cand : cand + 1, :]
+            real_cos = real_part * cosine
+            imag_sin = imag_part * sine_value
+            imag_cos = imag_part * cosine
+            real_sin = real_part * sine_value
+            put(cand, real_cos - imag_sin, imag_cos + real_sin)
+            put(cands - 1 - cand, real_cos + imag_sin, imag_cos - real_sin)
+    cross = lax.dot_general(
+        moved_ref[...],
+        weighted_ref[...],
+        (((1,), (1,)), ((), ())),
+        preferred_element_type=jnp.float32,
+    )
+    power = jnp.dot(
+        power_ref[...], hot_ref[...], precision=HIGH, preferred_element_type=jnp.float32
+    )
+    for tile in range(tiles):
+        half_power = 0.5 * power[tile * orients : (tile + 1) * orients]
+        named = [tiles_ref[j : j + 1, :] == step * tiles + tile for j in range(windows)]
+        for cand in range(cands):
+            first = tile * block + cand * orients
+            value = cross[first : first + orients] - half_power
+            rows = pl.ds(cand * orients, orients)
+            for j in range(windows):
+                chosen_ref[j, rows, :] = jnp.where(named[j], value, chosen_ref[j, rows, :])
+
+    @pl.when(step == pl.num_programs(0) - 1)
+    def _():
+        kept = orients // 2
+        used = cands * windows * kept
+        for j in range(windows):
+            start = starts_ref[j : j + 1, :]
+            for cand in range(cands):
+                value = chosen_ref[j, pl.ds(cand * orients, orients), :]
+                bit = orients // 2
+                while bit:
+                    turned = pltpu.roll(value, orients - bit, 0)
+                    value = jnp.where((start & bit) != 0, turned, value)
+                    bit //= 2
+                final_ref[pl.ds((cand * windows + j) * kept, kept), :] = value[:kept]
+        spare = final_ref.shape[0] - used
+        final_ref[pl.ds(used, spare), :] = jnp.zeros((spare, final_ref.shape[1]), jnp.float32)
+        turned = final_ref[...].T
+        column = lax.broadcasted_iota(jnp.int32, turned.shape, 1)
+        out_ref[...] = jnp.where(column >= used, energy_ref[...], turned)
+
+
+def exchange(values, tile_count):
+    rows, pair, band_width = values.shape
+    blocks = values.reshape(rows, pair, tile_count, band_width // tile_count)
+    blocks = jnp.transpose(blocks, (2, 1, 0, 3))
+    return lax.all_to_all(blocks, "tile", split_axis=0, concat_axis=0, tiled=True)
+
+
+def band_plan(particles, projections, noise_weight, tile_list, ori_start, shifts, defocus_bin):
+    tile_count = lax.axis_size("tile")
+    tile_index = lax.axis_index("tile")
+    band_index = lax.axis_index("shell")
+    local_count, pair, band_width = particles.shape
+    orients = projections.shape[0]
+    windows = tile_list.shape[1]
+    width = band_width // tile_count
+    lines = width // BOX
+    count = local_count * tile_count
+    cands = TSIDE * TSIDE
+
+    labels = jnp.concatenate([tile_list, ori_start, shifts, defocus_bin[:, None]], axis=1).T
+    labels = lax.all_gather(labels, "tile", axis=1, tiled=True)
+    part_in = exchange(particles, tile_count)
+    proj_in = exchange(projections, tile_count)
+
+    tiles_all = labels[:windows]
+    starts_all = labels[windows : 2 * windows]
+    shift_x = labels[2 * windows]
+    shift_y = labels[2 * windows + 1]
+    bins = labels[2 * windows + 2]
+
+    freq_x, freq_y = frequencies(band_index * band_width + tile_index * width, width)
+    weight = lax.dynamic_slice_in_dim(noise_weight, tile_index * width, width, 0)
+    ctf = ctf_table(freq_x, freq_y, NBIN)
+    factor = pick_rows(bins, weight[None, :] * ctf)
+    steps = jnp.arange(2 * SHIFT_MAX + 1, dtype=jnp.int32) - SHIFT_MAX
+    none = jnp.zeros((), jnp.int32)
+    own_y = jnp.arange(BOX, dtype=jnp.int32) - BOX // 2
+    own_x = freq_x[::BOX]
+    table_y = jnp.concatenate(rotation(own_y[None, :], own_y[None, :], none, steps[:, None]), axis=1)
+    table_x = jnp.concatenate(rotation(own_x[None, :], own_x[None, :], steps[:, None], none), axis=1)
+    wave_y = pick_rows(shift_y + SHIFT_MAX, table_y)
+    wave_x = pick_rows(shift_x + SHIFT_MAX, table_x)
+
+    weighted, energy = pl.pallas_call(
+        weigh_kernel,
+        grid=(tile_count,),
+        in_specs=[
+            pl.BlockSpec((1, pair, local_count, width), lambda i: (i, 0, 0, 0)),
+            pl.BlockSpec((local_count, width), lambda i: (i, 0)),
+            pl.BlockSpec((local_count, 2 * BOX), lambda i: (i, 0)),
+            pl.BlockSpec((local_count, 2 * lines), lambda i: (i, 0)),
+            pl.BlockSpec((1, width), lambda i: (0, 0)),
+        ],
+        out_specs=[
+            pl.BlockSpec((local_count, pair * width), lambda i: (i, 0)),
+            pl.BlockSpec((local_count, 1), lambda i: (i, 0)),
+        ],
+        out_shape=[
+            jax.ShapeDtypeStruct((count, pair * width), jnp.bfloat16),
+            jax.ShapeDtypeStruct((count, 1), jnp.float32),
+        ],
+        name="weigh",
+    )(part_in, factor, wave_y, wave_x, weight[None, :])
+
+    values = proj_in.astype(jnp.float32)
+    magnitude = values[:, 0] * values[:, 0] + values[:, 1] * values[:, 1]
+    power = lax.dot_general(
+        magnitude.reshape(tile_count * orients, width),
+        weight[None, :] * ctf * ctf,
+        (((1,), (1,)), ((), ())),
+        precision=HIGH,
+        preferred_element_type=jnp.float32,
+    )
+    hot = (jnp.arange(NBIN, dtype=jnp.int32)[:, None] == bins[None, :]).astype(jnp.float32)
+    offsets = jnp.arange(TSIDE, dtype=jnp.int32) - TSIDE // 2
+    cos_t, sin_t = rotation(
+        freq_x[None, :],
+        freq_y[None, :],
+        jnp.repeat(offsets, TSIDE)[:, None],
+        jnp.tile(offsets, TSIDE)[:, None],
+    )
+    group = 2 if tile_count % 2 == 0 else 1
+    used = cands * windows * (orients // 2)
+    columns = round_up(used + 1, 128)
+
+    def whole(*shape):
+        return pl.BlockSpec(shape, lambda i: (0,) * len(shape))
+
+    partial_value = pl.pallas_call(
+        functools.partial(score_kernel, orients),
+        grid=(tile_count // group,),
+        in_specs=[
+            pl.BlockSpec((group, pair, orients, width), lambda i: (i, 0, 0, 0)),
+            pl.BlockSpec((group * orients, NBIN), lambda i: (i, 0)),
+            whole(count, pair * width),
+            whole(count, 1),
+            whole(NBIN, count),
+            whole(windows, count),
+            whole(windows, count),
+            whole(cands, width),
+            whole(cands, width),
+        ],
+        out_specs=whole(count, columns),
+        out_shape=jax.ShapeDtypeStruct((count, columns), jnp.float32),
+        scratch_shapes=[
+            pltpu.VMEM((group * cands * orients, pair * width), jnp.bfloat16),
+            pltpu.VMEM((windows, cands * orients, count), jnp.float32),
+            pltpu.VMEM((columns, count), jnp.float32),
+        ],
+        compiler_params=pltpu.CompilerParams(vmem_limit_bytes=48 * 1024 * 1024),
+        name="score",
+    )(proj_in, power, weighted, energy, hot, tiles_all, starts_all, cos_t, sin_t)
+
+    blocks = partial_value.reshape(tile_count, local_count, columns)
+    blocks = lax.all_to_all(blocks, "tile", split_axis=0, concat_axis=0, tiled=True)
+    summed = jnp.sum(blocks, axis=0)
+    summed = jnp.sum(lax.all_gather(summed, "shell", axis=0), axis=0)
+    scores = summed[:, :used].reshape(local_count, cands, windows * (orients // 2))
+    return finish(scores, summed[:, used])
+
+
+def per_device(particles, projections, noise_weight, tile_list, ori_start, shifts, defocus_bin):
+    piece = BOX * lax.axis_size("tile")
+    plan = band_plan if particles.shape[2] % piece == 0 else slot_plan
+    return plan(
+        particles, projections, noise_weight, tile_list, ori_start, shifts, defocus_bin
+    )
+
+
 def solution(mesh):
     in_specs = (
         P("tile", None, "shell"),

time: 565 us -> 211 us (0.37); the launches traced: 555 us -> 211 us
  waiting for transfers between devices: 185 us -> 32.4 us
  other arithmetic: 141 us -> 2.64 us
  blocking collectives: 4.91 us -> 99.2 us
  starting transfers between devices: 83.9 us -> 18.8 us
  local copies, waits for them, and re-layouts: 81.7 us -> 18.8 us
  matrix products: 43.7 us -> 7.19 us
  Pallas kernels: 0 us -> 30.7 us
  between operations: 14.8 us -> 0.86 us
    all_to_all x3 -> x2, waiting for transfers between devices: 163 us -> 32.4 us  [exchange(): lax.all_to_all(blocks, 'tile', split_axis=0, concat_axis=0, tiled=True)]
    another operation x5 -> x0, other arithmetic: 87.1 us -> none  [the longest x1 46 us: shifted_tables(): stacked = jnp.stack([moved_real, moved_imag], axis=2).astype(jnp.bfloat16)]
    all_to_all x3 -> x2, starting transfers between devices: 83.9 us -> 18.8 us  [exchange(): lax.all_to_all(blocks, 'tile', split_axis=0, concat_axis=0, tiled=True)]
    all_gather x0 -> x2, blocking collectives: none -> 56.9 us  [the longest x1 50.9 us: band_plan(): labels = lax.all_gather(labels, 'tile', axis=1, tiled=True)]
    all_to_all x0 -> x1, blocking collectives: none -> 42.3 us  [band_plan(): lax.all_to_all(blocks, 'tile', split_axis=0, concat_axis=0, tiled=True)]
    gather x9 -> x0, local copies, waits for them, and re-layouts: 38.8 us -> none  [the longest x1 17.2 us: per_device(): jnp.take(weighted, particle, axis=0)]
    convert_element_type x3 -> x0, local copies, waits for them, and re-layouts: 32.9 us -> none  [the longest x1 32.7 us: shifted_tables(): stacked = jnp.stack([moved_real, moved_imag], axis=2).astype(jnp.bfloat16)]
    pallas_call x0 -> x2, Pallas kernels: none -> 30.7 us  [the longest x1 19.3 us: band_plan(): pl.pallas_call(functools.partial(score_kernel, orients), grid=(tile_count...]
  transfers between devices with their start and end apart: 4 -> 2, of which waited for: 3 -> 1; matrix products, arithmetic and copies ran while one was open for 34% -> 9% of each run, Pallas kernels for 0% -> 0%
where the time goes in v1:
time: 211 us
  blocking collectives  99.2 us (47%)
  waiting for transfers between devices  32.4 us (15%)
  Pallas kernels  30.7 us (15%)
  local copies, waits for them, and re-layouts  18.8 us (9%)
  starting transfers between devices  18.8 us (9%)
  matrix products  7.19 us (3%)
  other arithmetic  2.64 us (1%)
    all_gather x1, blocking collectives, band_plan(): labels = lax.all_gather(labels, 'tile', axis=1, tiled=True)  50.9 us
    all_to_all x1, blocking collectives, band_plan(): lax.all_to_all(blocks, 'tile', split_axis=0, concat_axis=0, tiled=True)  42.3 us
    all_to_all x2, waiting for transfers between devices, exchange(): lax.all_to_all(blocks, 'tile', split_axis=0, concat_axis=0, tiled=True)  32.4 us
    pallas_call x1, Pallas kernels, band_plan(): pl.pallas_call(functools.partial(score_kernel, orients), grid=(tile_count...  19.3 us
    all_to_all x2, starting transfers between devices, exchange(): lax.all_to_all(blocks, 'tile', split_axis=0, concat_axis=0, tiled=True)  18.8 us
    reshape x4, local copies, waits for them, and re-layouts, exchange(): blocks = values.reshape(rows, pair, tile_count, band_width // tile_count)  14.3 us
    pallas_call x1, Pallas kernels, band_plan(): pl.pallas_call(weigh_kernel, grid=(tile_count,), in_specs=[pl.BlockSpec((...  11.4 us
    all_gather x1, blocking collectives, band_plan(): summed = jnp.sum(lax.all_gather(summed, 'shell', axis=0), axis=0)  5.94 us
  transfers between devices with their start and end apart: 2, of which 1 were waited for; matrix products, arithmetic and copies ran while one was open for 9% of the time, Pallas kernels for 0%

profile of v1, /device:TPU:0, one launch (start us, length us, event | category | flops | bytes accessed | tf_op | source)
XLA Modules:
  0.0 210.6 jit_solution(5272137103027817426)
XLA Ops:
  0.6 3.3 %reshape.137 = bf16[32,2,16,1024]{3,2,1,0:T(8,128)(2,1)S(1)} reshape(bf16[32,2,16384]{2,1,0:T(2,128)(2,1)} %param.8) | data formatting | bytes 4194304 | tf_op jit(solution)/shard_map/reshape | solution.py:310
  3.9 2.5 %copy.55 = bf16[32,2,16,1024]{3,0,1,2:T(8,128)(2,1)} copy(bf16[32,2,16,1024]{3,2,1,0:T(8,128)(2,1)S(1)} %reshape.137) | data formatting | bytes 4194304 | tf_op jit(solution)/shard_map/reshape | solution.py:310
  6.4 7.4 %all-to-all-start = ((bf16[16,2,32,1024]{3,2,1,0:T(8,128)(2,1)}), bf16[16,2,32,1024]{3,2,1,0:T(8,128)(2,1)S(1)}, u32[]{:S(2)}, u32[]{:S(2)}) async-start(bf16[16,2,32,1024]{3,2,1,0:T(8,128)(2,1)} %bitcast.23), calls=%async_computation | async-start | bytes 4194304 | tf_op jit(solution)/shard_map/all_to_all | solution.py:312
  13.9 4.5 %reshape.138 = bf16[32,2,16,1024]{3,2,1,0:T(8,128)(2,1)} reshape(bf16[32,2,16384]{2,1,0:T(2,128)(2,1)} %param.7) | data formatting | bytes 4194304 | tf_op jit(solution)/shard_map/reshape | solution.py:310
  18.3 4.1 %copy.54 = bf16[32,2,16,1024]{3,0,1,2:T(8,128)(2,1)} copy(bf16[32,2,16,1024]{3,2,1,0:T(8,128)(2,1)} %reshape.138) | data formatting | bytes 4194304 | tf_op jit(solution)/shard_map/reshape | solution.py:310
  22.4 32.4 %all-to-all-done.proj_ref = bf16[16,2,32,1024]{3,2,1,0:T(8,128)(2,1)S(1)} async-done(((bf16[16,2,32,1024]{3,2,1,0:T(8,128)(2,1)}), bf16[16,2,32,1024]{3,2,1,0:T(8,128)(2,1)S(1)}, u32[]{:S(2)}, u32[]{:S(2)}) %all-to-all-start) | async-done | bytes 2097184 | tf_op jit(solution)/shard_map/all_to_all | solution.py:312
  54.8 0.0 copy-start.3
  54.8 0.0 copy-start.4
  54.8 0.0 copy-start.5
  54.8 0.0 copy-start.6
  54.8 11.4 %all-to-all-start.1 = ((bf16[16,2,32,1024]{3,2,1,0:T(8,128)(2,1)}), bf16[16,2,32,1024]{3,2,1,0:T(8,128)(2,1)}, u32[]{:S(2)}, u32[]{:S(2)}) async-start(bf16[16,2,32,1024]{3,2,1,0:T(8,128)(2,1)} %bitcast.22), calls=%async_computation.1 | async-start | bytes 4194304 | tf_op jit(solution)/shard_map/all_to_all | solution.py:312
  66.3 0.0 copy-done.3
  66.3 0.0 copy-done.4
  66.3 0.0 copy-done.5
  66.3 0.0 copy-done.6
  66.3 50.9 %all-gather.1 = s32[16,32,11]{1,2,0:T(8,128)S(1)} all-gather(s32[1,32,11]{1,2,0:T(8,128)S(1)} %add_bitcast_fusion), channel_id=1, replica_groups=mesh['tile'=16,'shell'=2] {'tile'}, dimensions={0}, use_global_device_ids=true | all-gather | bytes 23936 | tf_op jit(solution)/shard_map/all_gather | solution.py:328
  117.3 0.1 reshape.136
  117.4 0.1 slice.37
  117.5 0.1 mul.263
  117.6 0.1 broadcast_in_dim.8
  117.6 0.1 mul.259
  117.7 0.7 dynamic_slice.3
  118.5 0.1 fusion.51
  118.7 0.2 fusion.37
  118.8 0.3 fusion.15
  119.2 1.0 fusion.3.wave_x_ref
  120.2 1.6 fusion.2.wave_y_ref
  121.8 2.6 %fusion.1.factor_ref = f32[512,1024]{1,0:T(8,128)} fusion(s32[512]{0:T(512)S(1)} %bitcast.29, f32[1024]{0:T(1024)S(1)} %get-tuple-element.29, f32[1024]{0:T(1024)S(1)} %get-tuple-element.30, f32[1024]{0:T(1024)S(1)} %multiply_add_fusion, f32[16]{0:T(128)S(1)} %add_multiply_fusion, f32[1024]{0:T(1024)S(1)} %dynamic_slice.3), kind=kOutput, calls=%fused_computation.9 | convolution fusion | flops 100802560 | bytes 2115648 | tf_op jit(solution)/shard_map/dot_general | solution.py:57
  124.4 0.5 convert_element_type.46
  124.9 0.6 fusion
  125.5 0.0 copy-done.2
  125.5 2.0 fusion.8.power_ref
  127.5 0.0 all-to-all-done.1.part_ref
  127.5 11.4 %weigh.1 = (bf16[512,2048]{1,0:T(8,128)(2,1)}, f32[512,1]{1,0:T(8,128)}) custom-call(bf16[16,2,32,1024]{3,2,1,0:T(8,128)(2,1)} %all-to-all-done.1.part_ref, f32[512,1024]{1,0:T(8,128)} %fusion.1.factor_ref, f32[512,512]{1,0:T(8,128)} %fusion.2.wave_y_ref, f32[512,8]{1,0:T(8,128)} %fusion.3.wave_x_ref, f32[1,1024]{1,0:T(1,128)} %bitcast.27), custom_call_target="tpu_custom_call" | custom-call | tf_op jit(solution)/shard_map/weigh/pallas_call | solution.py:351
  138.9 1.6 copy-done
  140.5 0.9 copy-done.1
  141.5 19.3 %score.1 = f32[512,640]{1,0:T(8,128)S(1)} custom-call(bf16[16,2,32,1024]{3,2,1,0:T(8,128)(2,1)S(1)} %all-to-all-done.proj_ref, f32[512,16]{1,0:T(8,128)S(1)} %fusion.8.power_ref, bf16[512,2048]{1,0:T(8,128)(2,1)S(1)} %copy-done, f32[512,1]{1,0:T(8,128)S(1)} %copy-done.1, f32[16,512]{1,0:T(8,128)S(1)} %fusion.31.hot_ref, ...), custom_call_target="tpu_custom_call" | custom-call | tf_op jit(solution)/shard_map/score/pallas_call | solution.py:396
  160.8 42.3 %all_to_all.15 = f32[16,32,640]{2,1,0:T(8,128)S(1)} all-to-all(f32[16,32,640]{2,1,0:T(8,128)S(1)} %bitcast.20), channel_id=1, replica_groups=mesh['tile'=16,'shell'=2] {'tile'}, dimensions={0} | all-to-all | bytes 2621440 | tf_op jit(solution)/shard_map/all_to_all | solution.py:422
  203.1 0.1 reduce_sum.27
  203.1 5.9 %all-gather = f32[64,640]{1,0:T(8,128)S(1)} all-gather(f32[32,640]{1,0:T(8,128)S(1)} %reduce_sum.27), channel_id=2, replica_groups=mesh['tile'=16,'shell'=2] {'shell'}, dimensions={0}, use_global_device_ids=true | all-gather | bytes 245760 | tf_op jit(solution)/shard_map/all_gather | solution.py:424
  209.1 0.2 fusion.35
  209.3 0.2 subtract_reduce_fusion
  209.5 0.2 exponential_reduce_fusion
  209.7 0.1 reshape.133
  209.8 0.0 copy-start.7
  209.8 0.1 subtract_exponential_fusion
  209.9 0.7 copy.45
  210.6 0.0 copy-done.7
  (18 shorter events, 0.2 us)
Async XLA Ops:
  6.4 48.4 %all-to-all-start = ((bf16[16,2,32,1024]{3,2,1,0:T(8,128)(2,1)}), bf16[16,2,32,1024]{3,2,1,0:T(8,128)(2,1)S(1)}, u32[]{:S(2)}, u32[]{:S(2)}) async-start(bf16[16,2,32,1024]{3,2,1,0:T(8,128)(2,1)} %bitcast.23), calls=%async_computation | async-start | bytes 4194304 | tf_op jit(solution)/shard_map/all_to_all | solution.py:312
  54.8 11.4 %copy-start.3 = (s32[32,4]{0,1:T(4,128)S(1)}, s32[32,4]{0,1:T(4,128)}, u32[]{:S(2)}) copy-start(s32[32,4]{0,1:T(4,128)} %param.11) | copy-start | bytes 1540
  54.8 11.4 %copy-start.4 = (s32[32,4]{0,1:T(4,128)S(1)}, s32[32,4]{0,1:T(4,128)}, u32[]{:S(2)}) copy-start(s32[32,4]{0,1:T(4,128)} %param.10) | copy-start | bytes 1540
  54.8 11.5 %copy-start.5 = (s32[32,2]{0,1:T(2,128)S(1)}, s32[32,2]{0,1:T(2,128)}, u32[]{:S(2)}) copy-start(s32[32,2]{0,1:T(2,128)} %param.12) | copy-start | bytes 772
  54.8 11.5 %copy-start.6 = (s32[32]{0:T(128)S(1)}, s32[32]{0:T(128)}, u32[]{:S(2)}) copy-start(s32[32]{0:T(128)} %param.13) | copy-start | bytes 388
  54.8 72.7 %all-to-all-start.1 = ((bf16[16,2,32,1024]{3,2,1,0:T(8,128)(2,1)}), bf16[16,2,32,1024]{3,2,1,0:T(8,128)(2,1)}, u32[]{:S(2)}, u32[]{:S(2)}) async-start(bf16[16,2,32,1024]{3,2,1,0:T(8,128)(2,1)} %bitcast.22), calls=%async_computation.1 | async-start | bytes 4194304 | tf_op jit(solution)/shard_map/all_to_all | solution.py:312
  118.4 7.1 %copy-start.2 = (f32[1024]{0:T(1024)}, f32[1024]{0:T(1024)S(1)}, u32[]{:S(2)}) copy-start(f32[1024]{0:T(1024)S(1)} %dynamic_slice.3) | copy-start | bytes 12292
  138.9 1.6 copy-start
  140.5 0.9 copy-start.1
  209.8 0.9 copy-start.7

commit v2 on v1

--- a/solution.py
+++ b/solution.py
@@ -305,10 +305,13 @@
         out_ref[...] = jnp.where(column >= used, energy_ref[...], turned)
 
 
-def exchange(values, tile_count):
+def split_band(values, tile_count):
     rows, pair, band_width = values.shape
     blocks = values.reshape(rows, pair, tile_count, band_width // tile_count)
-    blocks = jnp.transpose(blocks, (2, 1, 0, 3))
+    return jnp.transpose(blocks, (2, 1, 0, 3))
+
+
+def exchange(blocks):
     return lax.all_to_all(blocks, "tile", split_axis=0, concat_axis=0, tiled=True)
 
 
@@ -326,8 +329,10 @@
 
     labels = jnp.concatenate([tile_list, ori_start, shifts, defocus_bin[:, None]], axis=1).T
     labels = lax.all_gather(labels, "tile", axis=1, tiled=True)
-    part_in = exchange(particles, tile_count)
-    proj_in = exchange(projections, tile_count)
+    part_blocks, labels = lax.optimization_barrier((split_band(particles, tile_count), labels))
+    part_in = exchange(part_blocks)
+    proj_blocks, part_in = lax.optimization_barrier((split_band(projections, tile_count), part_in))
+    proj_in = exchange(proj_blocks)
 
     tiles_all = labels[:windows]
     starts_all = labels[windows : 2 * windows]

time: 211 us -> 201 us (0.953)
  blocking collectives: 99.2 us -> 71.8 us
  waiting for transfers between devices: 32.4 us -> 54.8 us
  starting transfers between devices: 18.8 us -> 14.9 us
    all_gather x1, blocking collectives: 50.9 us -> 23.5 us  [band_plan(): labels = lax.all_gather(labels, 'tile', axis=1, tiled=True)]
    all_to_all x2, waiting for transfers between devices: 32.4 us -> 54.8 us  [exchange(): lax.all_to_all(blocks, 'tile', split_axis=0, concat_axis=0, tiled=True)]
    all_to_all x2, starting transfers between devices: 18.8 us -> 14.9 us  [exchange(): lax.all_to_all(blocks, 'tile', split_axis=0, concat_axis=0, tiled=True)]
  transfers between devices with their start and end apart: 2 -> 2, of which waited for: 1 -> 2; matrix products, arithmetic and copies ran while one was open for 9% -> 8% of each run, Pallas kernels for 0% -> 6%
where the time goes in v2:
time: 201 us
  blocking collectives  71.8 us (36%)
  waiting for transfers between devices  54.8 us (27%)
  Pallas kernels  30.7 us (15%)
  local copies, waits for them, and re-layouts  17.7 us (9%)
  starting transfers between devices  14.9 us (7%)
  matrix products  7.3 us (4%)
  other arithmetic  2.64 us (1%)
    all_to_all x2, waiting for transfers between devices, exchange(): lax.all_to_all(blocks, 'tile', split_axis=0, concat_axis=0, tiled=True)  54.8 us
    all_to_all x1, blocking collectives, band_plan(): lax.all_to_all(blocks, 'tile', split_axis=0, concat_axis=0, tiled=True)  42.4 us
    all_gather x1, blocking collectives, band_plan(): labels = lax.all_gather(labels, 'tile', axis=1, tiled=True)  23.5 us
    pallas_call x1, Pallas kernels, band_plan(): pl.pallas_call(functools.partial(score_kernel, orients), grid=(tile_count...  19.3 us
    all_to_all x2, starting transfers between devices, exchange(): lax.all_to_all(blocks, 'tile', split_axis=0, concat_axis=0, tiled=True)  14.9 us
    reshape x4, local copies, waits for them, and re-layouts, split_band(): blocks = values.reshape(rows, pair, tile_count, band_width // tile_count)  14.3 us
    pallas_call x1, Pallas kernels, band_plan(): pl.pallas_call(weigh_kernel, grid=(tile_count,), in_specs=[pl.BlockSpec((...  11.4 us
    all_gather x1, blocking collectives, band_plan(): summed = jnp.sum(lax.all_gather(summed, 'shell', axis=0), axis=0)  5.94 us
  transfers between devices with their start and end apart: 2, of which 2 were waited for; matrix products, arithmetic and copies ran while one was open for 8% of the time, Pallas kernels for 6%

profile of v2, /device:TPU:0, one launch (start us, length us, event | category | flops | bytes accessed | tf_op | source)
XLA Modules:
  0.0 200.7 jit_solution(10302939723997716042)
XLA Ops:
  0.6 3.3 %reshape.138 = bf16[32,2,16,1024]{3,2,1,0:T(8,128)(2,1)S(1)} reshape(bf16[32,2,16384]{2,1,0:T(2,128)(2,1)} %param.7) | data formatting | bytes 4194304 | tf_op jit(solution)/shard_map/reshape | solution.py:310
  3.9 0.0 copy-start.5
  3.9 0.0 copy-start.6
  4.0 0.0 copy-start.7
  4.0 0.0 copy-start.8
  4.0 2.5 %copy.54 = bf16[32,2,16,1024]{3,0,1,2:T(8,128)(2,1)} copy(bf16[32,2,16,1024]{3,2,1,0:T(8,128)(2,1)S(1)} %reshape.138) | data formatting | bytes 4194304 | tf_op jit(solution)/shard_map/reshape | solution.py:310
  6.4 0.0 copy-done.5
  6.4 0.0 copy-done.6
  6.4 0.0 copy-done.7
  6.4 0.0 copy-done.8
  6.5 23.5 %all-gather.1 = s32[16,32,11]{1,2,0:T(8,128)S(1)} all-gather(s32[1,32,11]{1,2,0:T(8,128)S(1)} %add_bitcast_fusion), channel_id=1, replica_groups=mesh['tile'=16,'shell'=2] {'tile'}, dimensions={0}, use_global_device_ids=true | all-gather | bytes 23936 | tf_op jit(solution)/shard_map/all_gather | solution.py:331
  30.0 0.1 reshape.136
  30.1 3.7 %all-to-all-start = ((bf16[16,2,32,1024]{3,2,1,0:T(8,128)(2,1)}), bf16[16,2,32,1024]{3,2,1,0:T(8,128)(2,1)S(1)}, u32[]{:S(2)}, u32[]{:S(2)}) async-start(bf16[16,2,32,1024]{3,2,1,0:T(8,128)(2,1)} %bitcast.23), calls=%async_computation | async-start | bytes 4194304 | tf_op jit(solution)/shard_map/all_to_all | solution.py:315
  33.8 4.5 %reshape.137 = bf16[32,2,16,1024]{3,2,1,0:T(8,128)(2,1)} reshape(bf16[32,2,16384]{2,1,0:T(2,128)(2,1)} %param.8) | data formatting | bytes 4194304 | tf_op jit(solution)/shard_map/reshape | solution.py:310
  38.3 4.1 %copy.55 = bf16[32,2,16,1024]{3,0,1,2:T(8,128)(2,1)} copy(bf16[32,2,16,1024]{3,2,1,0:T(8,128)(2,1)} %reshape.137) | data formatting | bytes 4194304 | tf_op jit(solution)/shard_map/reshape | solution.py:310
  42.4 32.4 %all-to-all-done.part_ref = bf16[16,2,32,1024]{3,2,1,0:T(8,128)(2,1)S(1)} async-done(((bf16[16,2,32,1024]{3,2,1,0:T(8,128)(2,1)}), bf16[16,2,32,1024]{3,2,1,0:T(8,128)(2,1)S(1)}, u32[]{:S(2)}, u32[]{:S(2)}) %all-to-all-start) | async-done | bytes 2097184 | tf_op jit(solution)/shard_map/all_to_all | solution.py:315
  74.7 1.3 copy-done.2
  76.0 11.2 %all-to-all-start.1 = ((bf16[16,2,32,1024]{3,2,1,0:T(8,128)(2,1)}), bf16[16,2,32,1024]{3,2,1,0:T(8,128)(2,1)S(1)}, u32[]{:S(2)}, u32[]{:S(2)}) async-start(bf16[16,2,32,1024]{3,2,1,0:T(8,128)(2,1)} %bitcast.22), calls=%async_computation.1 | async-start | bytes 4194304 | tf_op jit(solution)/shard_map/all_to_all | solution.py:315
  87.3 0.1 slice.37
  87.4 0.1 mul.263
  87.5 0.1 broadcast_in_dim.8
  87.5 0.1 mul.259
  87.6 0.7 dynamic_slice.3
  88.4 0.1 fusion.51
  88.5 0.2 fusion.37
  88.7 0.3 fusion.15
  89.1 1.0 fusion.3.wave_x_ref
  90.1 1.7 fusion.2.wave_y_ref
  91.8 2.6 %fusion.1.factor_ref = f32[512,1024]{1,0:T(8,128)} fusion(s32[512]{0:T(512)S(1)} %bitcast.29, f32[1024]{0:T(1024)S(1)} %get-tuple-element.37, f32[1024]{0:T(1024)S(1)} %get-tuple-element.38, f32[1024]{0:T(1024)S(1)} %multiply_add_fusion, f32[16]{0:T(128)S(1)} %add_multiply_fusion, f32[1024]{0:T(1024)S(1)} %dynamic_slice.3), kind=kOutput, calls=%fused_computation.9 | convolution fusion | flops 100802560 | bytes 2115648 | tf_op jit(solution)/shard_map/dot_general | solution.py:57
  94.4 11.4 %weigh.1 = (bf16[512,2048]{1,0:T(8,128)(2,1)}, f32[512,1]{1,0:T(8,128)}) custom-call(bf16[16,2,32,1024]{3,2,1,0:T(8,128)(2,1)} %copy-done.2, f32[512,1024]{1,0:T(8,128)} %fusion.1.factor_ref, f32[512,512]{1,0:T(8,128)} %fusion.2.wave_y_ref, f32[512,8]{1,0:T(8,128)} %fusion.3.wave_x_ref, f32[1,1024]{1,0:T(1,128)} %bitcast.27), custom_call_target="tpu_custom_call" | custom-call | tf_op jit(solution)/shard_map/weigh/pallas_call | solution.py:356
  105.8 22.4 %all-to-all-done.1.proj_ref = bf16[16,2,32,1024]{3,2,1,0:T(8,128)(2,1)S(1)} async-done(((bf16[16,2,32,1024]{3,2,1,0:T(8,128)(2,1)}), bf16[16,2,32,1024]{3,2,1,0:T(8,128)(2,1)S(1)}, u32[]{:S(2)}, u32[]{:S(2)}) %all-to-all-start.1) | async-done | bytes 2097184 | tf_op jit(solution)/shard_map/all_to_all | solution.py:315
  128.2 0.5 convert_element_type.46
  128.7 0.0 copy-start.4
  128.7 0.6 fusion
  129.4 0.0 copy-done.4
  129.4 2.0 fusion.8.power_ref
  131.4 19.3 %score.1 = f32[512,640]{1,0:T(8,128)S(1)} custom-call(bf16[16,2,32,1024]{3,2,1,0:T(8,128)(2,1)S(1)} %all-to-all-done.1.proj_ref, f32[512,16]{1,0:T(8,128)S(1)} %fusion.8.power_ref, bf16[512,2048]{1,0:T(8,128)(2,1)S(1)} %copy-done, f32[512,1]{1,0:T(8,128)S(1)} %copy-done.1, f32[16,512]{1,0:T(8,128)S(1)} %fusion.31.hot_ref, ...), custom_call_target="tpu_custom_call" | custom-call | tf_op jit(solution)/shard_map/score/pallas_call | solution.py:401
  150.7 42.4 %all_to_all.15 = f32[16,32,640]{2,1,0:T(8,128)S(1)} all-to-all(f32[16,32,640]{2,1,0:T(8,128)S(1)} %bitcast.20), channel_id=1, replica_groups=mesh['tile'=16,'shell'=2] {'tile'}, dimensions={0} | all-to-all | bytes 2621440 | tf_op jit(solution)/shard_map/all_to_all | solution.py:427
  193.1 0.1 reduce_sum.27
  193.1 5.9 %all-gather = f32[64,640]{1,0:T(8,128)S(1)} all-gather(f32[32,640]{1,0:T(8,128)S(1)} %reduce_sum.27), channel_id=2, replica_groups=mesh['tile'=16,'shell'=2] {'shell'}, dimensions={0}, use_global_device_ids=true | all-gather | bytes 245760 | tf_op jit(solution)/shard_map/all_gather | solution.py:429
  199.1 0.2 fusion.35
  199.3 0.2 subtract_reduce_fusion
  199.5 0.2 exponential_reduce_fusion
  199.7 0.1 reshape.133
  199.8 0.0 copy-start.9
  199.8 0.1 subtract_exponential_fusion
  199.9 0.7 copy.45
  200.7 0.0 copy-done.9
  (22 shorter events, 0.2 us)
Async XLA Ops:
  3.9 2.5 %copy-start.5 = (s32[32,4]{0,1:T(4,128)S(1)}, s32[32,4]{0,1:T(4,128)}, u32[]{:S(2)}) copy-start(s32[32,4]{0,1:T(4,128)} %param.11) | copy-start | bytes 1540
  3.9 2.5 %copy-start.6 = (s32[32,4]{0,1:T(4,128)S(1)}, s32[32,4]{0,1:T(4,128)}, u32[]{:S(2)}) copy-start(s32[32,4]{0,1:T(4,128)} %param.10) | copy-start | bytes 1540
  4.0 2.5 %copy-start.7 = (s32[32,2]{0,1:T(2,128)S(1)}, s32[32,2]{0,1:T(2,128)}, u32[]{:S(2)}) copy-start(s32[32,2]{0,1:T(2,128)} %param.12) | copy-start | bytes 772
  4.0 2.5 %copy-start.8 = (s32[32]{0:T(128)S(1)}, s32[32]{0:T(128)}, u32[]{:S(2)}) copy-start(s32[32]{0:T(128)} %param.13) | copy-start | bytes 388
  30.1 44.7 %all-to-all-start = ((bf16[16,2,32,1024]{3,2,1,0:T(8,128)(2,1)}), bf16[16,2,32,1024]{3,2,1,0:T(8,128)(2,1)S(1)}, u32[]{:S(2)}, u32[]{:S(2)}) async-start(bf16[16,2,32,1024]{3,2,1,0:T(8,128)(2,1)} %bitcast.23), calls=%async_computation | async-start | bytes 4194304 | tf_op jit(solution)/shard_map/all_to_all | solution.py:315
  74.7 1.3 copy-start.2
  76.0 52.2 %all-to-all-start.1 = ((bf16[16,2,32,1024]{3,2,1,0:T(8,128)(2,1)}), bf16[16,2,32,1024]{3,2,1,0:T(8,128)(2,1)S(1)}, u32[]{:S(2)}, u32[]{:S(2)}) async-start(bf16[16,2,32,1024]{3,2,1,0:T(8,128)(2,1)} %bitcast.22), calls=%async_computation.1 | async-start | bytes 4194304 | tf_op jit(solution)/shard_map/all_to_all | solution.py:315
  88.3 6.1 %copy-start.3 = (f32[1024]{0:T(1024)}, f32[1024]{0:T(1024)S(1)}, u32[]{:S(2)}) copy-start(f32[1024]{0:T(1024)S(1)} %dynamic_slice.3) | copy-start | bytes 12292
  128.7 0.7 copy-start.4
  129.3 2.0 %copy-start = (bf16[512,2048]{1,0:T(8,128)(2,1)S(1)}, bf16[512,2048]{1,0:T(8,128)(2,1)}, u32[]{:S(2)}) copy-start(bf16[512,2048]{1,0:T(8,128)(2,1)} %get-tuple-element.12.weighted_ref) | copy-start | bytes 6291460
  129.4 2.0 %copy-start.1 = (f32[512,1]{1,0:T(8,128)S(1)}, f32[512,1]{1,0:T(8,128)}, u32[]{:S(2)}) copy-start(f32[512,1]{1,0:T(8,128)} %get-tuple-element.13.energy_ref) | copy-start | bytes 6148
  199.8 0.9 copy-start.9
